TPU v7x, 128 devices: a whole 4x4x4 slice. The times are simulated.
128 devices in a mesh: dp: 16 (over y, x), mp: 8 (over z, core).
Axes of the slice: x: 4, y: 4, z: 4, core: 2. Of those that a mesh axis runs over, the one named last changes fastest.
Arguments:
- tokens: bfloat16 [65536, 1024], P(('dp', 'mp')), may hold values from -6 to 6
- norm_gain: float32 [2, 1024], replicated, may hold values from 0.1 to 1.9
- qkv_weight: bfloat16 [3, 1024, 1024], P(None, 'dp', 'mp')
- out_weight: bfloat16 [1024, 1024], P('mp', 'dp'), may hold values from -0.1875 to 0.1875
- variate_bias: float32 [2, 16], replicated, may hold values from -6 to 6
- ffn_weight: bfloat16 [2, 1024, 2816], P(None, 'dp', 'mp'), may hold values from -0.1875 to 0.1875
- down_weight: bfloat16 [2816, 1024], P('mp', 'dp'), may hold values from -0.109375 to 0.109375
- sample_ids: int32 [65536], P(('dp', 'mp')), may hold values from 0 to 127, as said below
- variate_ids: int32 [65536], P(('dp', 'mp')), may hold values from 0 to 15, as said below
- time_ids: int32 [65536], P(('dp', 'mp')), may hold values from 0 to 31, as said below
Outputs:
- encoded: bfloat16 [65536, 1024], P(('dp', 'mp'))
Inputs may be any that keep to these rules, and one draw needn't show every extreme that they name: `sample_ids`: within each packed sequence of 512 tokens the series numbers start at 0 and never fall; a series with v variates (1 to 16) and p patches (4 to 32) holds v * p consecutive tokens, the last series of a sequence may be cut short; some packed sequence holds 128 series of one variate and four patches each. `variate_ids`: A token's offset within its series divided by that series' patch count p. `time_ids`: A token's offset within its series modulo that series' patch count p.
All inputs are finite; a program needn't handle non-finite values.
Results may differ from a plain program's by a relative error of at most 0.017.
Values may be sent and summed in bfloat16 or wider, within the bound.
A program may use at most 128 MiB of HBM per device.

v0:
```python
import functools

import jax
import jax.numpy as jnp
import numpy as np
from jax import lax
from jax.experimental import pallas as pl
from jax.experimental.pallas import tpu as pltpu
from jax.sharding import PartitionSpec as P

L = 512
D = 1024
TIMES = 32
LOG2E = 1.4426950408889634
BF = jnp.bfloat16
F32 = jnp.float32
MESH = pl.DeviceIdType.MESH

A, B, C = 0, 1, 2
ORDERS = (("x", "y", "z"), ("y", "z", "x"), ("z", "x", "y"))
OUT_ROWS = (32, 16, 16)
OUT_AT = (0, 32, 48)
ROWS = ((64, 64, 64), tuple(128 + r for r in OUT_ROWS), (64, 64, 64))
HALF = ((32, 32, 32), (80, 80, 80), (32, 32, 32))
B_AT = (0, 160, 304)
OWN = 24


class Exchange:
    def __init__(self, bufs, send, recv):
        self.bufs, self.send, self.recv = bufs, send, recv
        dp, mp = lax.axis_index("dp"), lax.axis_index("mp")
        self.pos = {"x": lax.rem(dp, 4), "y": dp // 4, "z": mp // 2}
        self.core = lax.rem(mp, 2)
        self.started = []

    def device(self, axis=None, step=0):
        pos = dict(self.pos)
        core = self.core
        if axis == "core":
            core = 1 - core
        elif axis is not None:
            pos[axis] = lax.rem(pos[axis] + step + 4, 4)
        return (pos["y"] * 4 + pos["x"], pos["z"] * 2 + core)

    def slab(self, b, c, phase, shift, half):
        a1, a2, a3 = ORDERS[c]
        at = {k: self.pos[k] for k in "xyz"}
        axis = ORDERS[c][phase]
        at[axis] = lax.rem(at[axis] + shift + 4, 4)
        buf = self.bufs[b][c]
        base = self.core * 64 + at[a3] * 16
        if phase == 0:
            first = base + at[a2] * 4 + at[a1]
            top = HALF[b][c]
            rows = pl.ds(0, top) if half == 0 else pl.ds(top, ROWS[b][c] - top)
            return buf.at[pl.ds(first, 1), rows]
        if phase == 1:
            return buf.at[pl.ds(base + at[a2] * 4 + 2 * half, 2)]
        return buf.at[pl.ds(base + 8 * half, 8)]

    def copy(self, ref, b, c, slot, device):
        return pltpu.make_async_remote_copy(
            src_ref=ref,
            dst_ref=ref,
            send_sem=self.send.at[b, c, slot],
            recv_sem=self.recv.at[b, c, slot],
            device_id=device,
            device_id_type=MESH,
        )

    def start(self, b, c, slot, ref, device):
        copy = self.copy(ref, b, c, slot, device)
        copy.start()
        self.started.append(copy)

    def first(self, b, c, p):
        axis = ORDERS[c][p]
        for slot, half, step in ((0, 0, 1), (2, 1, -1), (1, 1, 1), (3, 0, -1)):
            self.start(b, c, p * 6 + slot, self.slab(b, c, p, 0, half), self.device(axis, step))

    def landed(self, b, c, p, slot):
        half = (0, 1, 1, 0, 0, 1)[slot]
        shift = (-1, -1, 1, 1, -2, 2)[slot]
        ref = self.slab(b, c, p, shift, half)
        self.copy(ref, b, c, p * 6 + slot, self.device(ORDERS[c][p], 1)).wait_recv()
        return ref

    def forward(self, b, c, p):
        axis = ORDERS[c][p]
        for slot, step in ((0, 1), (2, -1)):
            ref = self.landed(b, c, p, slot)
            self.start(b, c, p * 6 + 4 + slot // 2, ref, self.device(axis, step))
            if p == 2:
                self.share(b, c, slot, ref)

    def finish(self, b, c, p, slots=(1, 3, 4, 5)):
        for slot in slots:
            ref = self.landed(b, c, p, slot)
            if p == 2:
                self.share(b, c, slot, ref)

    def share(self, b, c, slot, ref):
        self.start(b, c, 18 + slot, ref, self.device("core"))

    def plane(self, b, c, core):
        return self.bufs[b][c].at[pl.ds(core * 64 + self.pos[ORDERS[c][2]] * 16, 16)]

    def share_own(self, b, c):
        self.start(b, c, OWN, self.plane(b, c, self.core), self.device("core"))

    def shared(self, b, c):
        other = self.device("core")
        self.copy(self.plane(b, c, self.core), b, c, OWN, other).wait_recv()
        for slot in range(6):
            ref = self.slab(b, c, 2, (-1, -1, 1, 1, -2, 2)[slot], (0, 1, 1, 0, 0, 1)[slot])
            self.copy(ref, b, c, 18 + slot, other).wait_recv()

    def every(self, action, b, p):
        for c in range(3):
            action(b, c, p)


def nt(a, b):
    return lax.dot_general(a, b, (((1,), (1,)), ((), ())), preferred_element_type=F32)


def nn(a, b):
    return jnp.dot(a, b, preferred_element_type=F32)


def spot(c, core, x, y, z):
    at = {"x": x, "y": y, "z": z}
    a1, a2, a3 = ORDERS[c]
    return core * 64 + at[a3] * 16 + at[a2] * 4 + at[a1]


def normed_into(dst, src, gain, row):
    g = gain[pl.ds(row, 1), :]

    def block(i, _):
        rows = pl.ds(pl.multiple_of(i * 64, 64), 64)
        wide = src[rows, :].astype(F32)
        square = jnp.mean(wide * wide, axis=-1, keepdims=True)
        dst[rows, :] = (wide * lax.rsqrt(square + 1e-05) * g).astype(BF)
        return 0

    lax.fori_loop(0, 8, block, 0)


def kernel(
    tok, gain, qkvw, packb, packc, table, slope, sids, vids, tids,
    out,
    a0, a1, a2, b0, b1, b2, c0, c1, c2,
    xn, same, away, cq, sq, ck, sk, qs, ks, vs, att, res, hid,
    stage, send, recv,
):
    ex = Exchange(((a0, a1, a2), (b0, b1, b2), (c0, c1, c2)), send, recv)

    def source(b, c):
        if b == A:
            return qkvw.at[c]
        if b == B:
            return packb.at[pl.ds(B_AT[c], ROWS[B][c])]
        return packc.at[c]

    def own(b, c):
        first = spot(c, ex.core, ex.pos["x"], ex.pos["y"], ex.pos["z"])
        return pltpu.make_async_copy(source(b, c), ex.bufs[b][c].at[first], stage.at[b, c])

    for b in (A, B, C):
        for c in range(3):
            own(b, c).start()
    barrier = pltpu.get_barrier_semaphore()
    for axis in "xyz":
        for step in (1, -1):
            pl.semaphore_signal(barrier, inc=1, device_id=ex.device(axis, step), device_id_type=MESH)
    pl.semaphore_signal(barrier, inc=1, device_id=ex.device("core"), device_id_type=MESH)
    pl.semaphore_wait(barrier, 7)

    for b in (A, B, C):
        for c in range(3):
            own(b, c).wait()
        ex.every(ex.first, b, 0)

    normed_into(xn, tok, gain, 0)
    for b in (A, B, C):
        ex.every(ex.forward, b, 0)

    eye = (
        lax.broadcasted_iota(jnp.int32, (L, L), 0) == lax.broadcasted_iota(jnp.int32, (L, L), 1)
    ).astype(F32).astype(BF)

    def column(ids):
        row = jnp.broadcast_to(ids[...].astype(F32), (128, L)).astype(BF)
        return nt(eye, row)

    def matches(ids):
        col = column(ids)
        row = jnp.broadcast_to(ids[...].astype(F32), (L, L))
        return jnp.concatenate([col] * 4, axis=1) == row

    same[...] = jnp.where(matches(vids), 1.0, 0.0)
    away[...] = jnp.where(matches(sids), 0.0, -1e30)

    ex.every(ex.finish, A, 0)
    ex.every(ex.first, A, 1)
    ex.every(ex.finish, C, 0)
    ex.every(ex.first, C, 1)

    lanes = lax.broadcasted_iota(jnp.int32, (L, 128), 1).astype(F32)
    hot = jnp.where(column(tids) == lanes, 1.0, 0.0).astype(BF)
    turn = nn(hot, table[...])
    cos = turn[:, 0:128] + turn[:, 256:384] + turn[:, 512:640]
    sin = turn[:, 128:256] + turn[:, 384:512] + turn[:, 640:768]
    cq[...] = cos * (LOG2E / 8.0)
    sq[...] = sin * (LOG2E / 8.0)
    ck[...] = cos
    sk[...] = sin

    ex.every(ex.forward, A, 1)
    ex.every(ex.finish, B, 0)
    ex.every(ex.finish, A, 1)
    ex.every(ex.first, A, 2)
    for c in range(3):
        ex.share_own(A, c)
    ex.every(ex.first, B, 1)
    ex.every(ex.forward, C, 1)
    ex.every(ex.finish, C, 1)
    ex.every(ex.forward, A, 2)
    ex.every(ex.forward, B, 1)
    ex.every(ex.finish, B, 1)
    ex.every(ex.first, B, 2)
    for c in range(3):
        ex.share_own(B, c)
    for c in range(3):
        ex.share_own(C, c)
    ex.every(ex.finish, A, 2)
    for c in range(3):
        ex.shared(A, c)

    def columns(b, c, z, rows):
        sides = []
        for core in range(2):
            parts = [
                ex.bufs[b][c][spot(c, core, x, y, z), rows, :]
                for y in range(4)
                for x in range(4)
            ]
            sides.append(jnp.concatenate(parts, axis=0))
        return jnp.concatenate(sides, axis=1)

    def turned(raw, cosine, sine):
        lane = lax.rem(lax.broadcasted_iota(jnp.int32, (L, 128), 1), 64)
        done = []
        for t in range(2):
            v = raw[:, t * 128 : (t + 1) * 128]
            other = jnp.where(lane < 32, pltpu.roll(v, 96, 1), pltpu.roll(v, 32, 1))
            done.append(v * cosine[...] + other * sine[...])
        return jnp.concatenate(done, axis=1).astype(BF)

    def group(z):
        every = slice(0, 64)
        qs[...] = turned(nn(xn[...], columns(A, 0, z, every)), cq, sq)
        ks[...] = turned(nn(xn[...], columns(A, 1, z, every)), ck, sk)
        vs[...] = nn(xn[...], columns(A, 2, z, every)).astype(BF)

        def head(h, _):
            mine = lax.broadcasted_iota(jnp.int32, (L, 256), 1) // 64 == h
            q = jnp.where(mine, qs[...], jnp.zeros((), BF))
            s = nt(q, ks[...]) + same[...] * slope[z * 4 + h] + away[...]
            e = jnp.exp2(s - jnp.max(s, axis=1, keepdims=True))
            total = jnp.sum(e, axis=1, keepdims=True)
            got = (nn(e.astype(BF), vs[...]) * (1.0 / total)).astype(BF)
            here = pl.ds(z * 256, 256)
            att[:, here] = jnp.where(mine, got, att[:, here])
            return 0

        lax.fori_loop(0, 4, head, 0)

    att[...] = jnp.zeros_like(att)
    group(0)
    group(1)
    ex.every(ex.forward, B, 2)
    ex.every(ex.first, C, 2)
    group(2)
    group(3)
    ex.every(functools.partial(ex.finish, slots=(1, 3)), B, 2)

    def project(y, _):
        tall = []
        for z in range(4):
            for core in range(2):
                parts = [
                    ex.bufs[B][c][spot(c, core, x, y, z), 0 : OUT_ROWS[c], :]
                    for x in range(4)
                    for c in range(3)
                ]
                tall.append(jnp.concatenate(parts, axis=0))
        here = pl.ds(pl.multiple_of(y * 256, 256), 256)
        mixed = nt(att[...], jnp.concatenate(tall, axis=1))
        res[:, here] = (tok[:, here].astype(F32) + mixed).astype(BF)
        return 0

    ex.every(functools.partial(ex.finish, slots=(4, 5)), B, 2)
    for c in range(3):
        ex.shared(B, c)
    lax.fori_loop(0, 4, project, 0)
    normed_into(xn, res, gain, 1)

    def feed(z, _):
        for c in range(3):
            r = OUT_ROWS[c]
            gate = nn(xn[...], columns(B, c, z, slice(r, r + 64)))
            up = nn(xn[...], columns(B, c, z, slice(r + 64, r + 128)))
            wide = gate / (1.0 + jnp.exp(-gate)) * up
            hid[:, pl.ds(pl.multiple_of(z * 768 + c * 256, 256), 256)] = wide.astype(BF)
        return 0

    lax.fori_loop(0, 2, feed, 0)
    ex.every(ex.forward, C, 2)
    lax.fori_loop(2, 4, feed, 0)
    ex.every(ex.finish, C, 2)
    for c in range(3):
        ex.shared(C, c)

    def down(y, _):
        wide = []
        for z in range(4):
            for c in range(3):
                for core in range(2):
                    parts = [ex.bufs[C][c][spot(c, core, x, y, z)] for x in range(4)]
                    wide.append(jnp.concatenate(parts, axis=0))
        here = pl.ds(pl.multiple_of(y * 256, 256), 256)
        fed = nt(hid[...], jnp.concatenate(wide, axis=1))
        out[:, here] = (res[:, here].astype(F32) + fed).astype(BF)
        return 0

    lax.fori_loop(0, 4, down, 0)
    for copy in ex.started:
        copy.wait_send()


def turn_table():
    freq = 10000.0 ** (-np.arange(32) / 32.0)
    angle = np.arange(TIMES)[:, None] * freq[None, :]
    cos = np.tile(np.cos(angle), (1, 4))
    sin = np.sin(angle)
    sin = np.tile(np.concatenate([-sin, sin], axis=1), (1, 2))
    left = np.concatenate([cos, sin], axis=1).astype(np.float32)
    terms = []
    for _ in range(3):
        term = left.astype(BF)
        terms.append(term)
        left = left - term.astype(np.float32)
    rows = np.concatenate(terms, axis=1)
    return np.concatenate([rows, np.zeros((128 - TIMES, rows.shape[1]), BF)], axis=0)


def local(
    tokens,
    norm_gain,
    qkv_weight,
    out_weight,
    variate_bias,
    ffn_weight,
    down_weight,
    sample_ids,
    variate_ids,
    time_ids,
):
    wide = jnp.pad(ffn_weight, ((0, 0), (0, 0), (0, 32)))
    turned_out = out_weight.T
    packb = jnp.concatenate(
        [
            piece
            for c in range(3)
            for piece in (
                turned_out[OUT_AT[c] : OUT_AT[c] + OUT_ROWS[c]],
                wide[0, :, c * 128 : (c + 1) * 128],
                wide[1, :, c * 128 : (c + 1) * 128],
            )
        ],
        axis=0,
    )
    tall = jnp.pad(down_weight, ((0, 32), (0, 0))).T
    packc = tall.reshape(64, 3, 128).transpose(1, 0, 2)
    slope = (variate_bias[0] - variate_bias[1]) * LOG2E
    vmem = pl.BlockSpec(memory_space=pltpu.VMEM)
    hbm = pl.BlockSpec(memory_space=pl.ANY)
    smem = pl.BlockSpec(memory_space=pltpu.SMEM)
    buffers = [
        pltpu.VMEM((128, ROWS[b][c], 128), BF) for b in (A, B, C) for c in range(3)
    ]
    return pl.pallas_call(
        kernel,
        out_shape=jax.ShapeDtypeStruct((L, D), BF),
        in_specs=[vmem, vmem, hbm, hbm, hbm, vmem, smem, vmem, vmem, vmem],
        out_specs=vmem,
        scratch_shapes=buffers
        + [
            pltpu.VMEM((L, D), BF),
            pltpu.VMEM((L, L), F32),
            pltpu.VMEM((L, L), F32),
            pltpu.VMEM((L, 128), F32),
            pltpu.VMEM((L, 128), F32),
            pltpu.VMEM((L, 128), F32),
            pltpu.VMEM((L, 128), F32),
            pltpu.VMEM((L, 256), BF),
            pltpu.VMEM((L, 256), BF),
            pltpu.VMEM((L, 256), BF),
            pltpu.VMEM((L, D), BF),
            pltpu.VMEM((L, D), BF),
            pltpu.VMEM((L, 3072), BF),
            pltpu.SemaphoreType.DMA((3, 3)),
            pltpu.SemaphoreType.DMA((3, 3, 25)),
            pltpu.SemaphoreType.DMA((3, 3, 25)),
        ],
        compiler_params=pltpu.CompilerParams(
            collective_id=0, has_side_effects=True, vmem_limit_bytes=67000000
        ),
    )(
        tokens,
        norm_gain,
        qkv_weight,
        packb,
        packc,
        jnp.asarray(turn_table()),
        slope,
        sample_ids.reshape(1, L),
        variate_ids.reshape(1, L),
        time_ids.reshape(1, L),
    )


def solution(mesh):
    return jax.shard_map(
        local,
        mesh=mesh,
        in_specs=(
            P(("dp", "mp"), None),
            P(),
            P(None, "dp", "mp"),
            P("mp", "dp"),
            P(),
            P(None, "dp", "mp"),
            P("mp", "dp"),
            P(("dp", "mp")),
            P(("dp", "mp")),
            P(("dp", "mp")),
        ),
        out_specs=P(("dp", "mp"), None),
        check_vma=False,
    )
```

profile of v0, /device:TPU:1, one launch (start us, length us, event | category | flops | bytes accessed | tf_op | source)
XLA Modules:
  0.0 109.0 jit_solution(17481543102969441263)
XLA Ops:
  0.0 0.0 copy-start
  0.0 1.3 %multiply_bitcast_fusion.slope = f32[16]{0:T(128)} fusion(f32[2,16]{1,0:T(2,128)} %param.15), kind=kLoop, calls=%fused_computation.15 | loop fusion | flops 32 | bytes 192 | tf_op jit(solution)/shard_map/mul | solution.py:388
  1.3 1.4 %bitcast_bitcast_fusion.packc = bf16[3,64,128]{2,1,0:T(8,128)(2,1)} fusion(bf16[352,64]{0,1:T(8,128)(2,1)} %param.17), kind=kLoop, calls=%fused_computation.2 | loop fusion | bytes 94208 | tf_op jit(solution)/shard_map/transpose | solution.py:387
  2.8 1.3 %constant_dynamic-update-slice_fusion.8 = bf16[448,128]{1,0:T(8,128)(2,1)} fusion(bf16[64,128]{1,0:T(8,128)(2,1)} %bitcast.30), kind=kLoop, calls=%fused_computation.12 | loop fusion | bytes 16384
  4.1 0.0 copy-done
  4.1 0.6 constant_dynamic-update-slice_fusion.7
  4.7 0.0 copy-start.1
  4.7 0.6 constant_dynamic-update-slice_fusion.6
  5.3 0.1 copy-done.1
  5.4 0.6 constant_dynamic-update-slice_fusion.5
  6.0 0.6 constant_dynamic-update-slice_fusion.4
  6.6 0.6 constant_dynamic-update-slice_fusion.3
  7.2 0.6 constant_dynamic-update-slice_fusion.2
  7.8 0.6 constant_dynamic-update-slice_fusion.1
  8.4 0.6 constant_dynamic-update-slice_fusion.packb
  9.0 97.7 %shard_map.109 = bf16[512,1024]{1,0:T(8,128)(2,1)} custom-call(bf16[512,1024]{1,0:T(8,128)(2,1)} %tok.1, f32[2,1024]{1,0:T(2,128)} %gain.1, bf16[3,64,128]{2,1,0:T(8,128)(2,1)} %qkvw.1, bf16[448,128]{1,0:T(8,128)(2,1)} %constant_dynamic-update-slice_fusion.packb, bf16[3,64,128]{2,1,0:T(8,128)(2,1)} %bitcast_bitcast_fusion.packc, ...), custom_call_target="tpu_custom_call" | custom-call | tf_op jit(solution)/shard_map/pallas_call | solution.py:395
  106.7 2.3 %copy.24 = bf16[512,1024]{1,0:T(8,128)(2,1)} copy(bf16[512,1024]{1,0:T(8,128)(2,1)} %shard_map.109) | data formatting | bytes 2097152
Async XLA Ops:
  0.0 4.1 %copy-start = (bf16[2,64,352]{2,1,0:T(8,128)(2,1)S(1)}, bf16[2,64,352]{2,1,0:T(8,128)(2,1)}, u32[]{:S(2)}) copy-start(bf16[2,64,352]{2,1,0:T(8,128)(2,1)} %param.16) | copy-start | bytes 270340
  4.7 0.7 copy-start.1
where the time goes:
time: 109 us
  Pallas kernels  97.7 us (90%)
  local copies, waits for them, and re-layouts  9.95 us (9%)
  other arithmetic  1.34 us (1%)
    pallas_call x1, Pallas kernels, local(): pl.pallas_call(kernel, out_shape=jax.ShapeDtypeStruct((L, D), BF), in_spe...  97.7 us
    unnamed x13, local copies, waits for them, and re-layouts  7.9 us

commit v1 on v0

v1 whole, which is shorter than its diff:
```python
import jax
import jax.numpy as jnp
import numpy as np
from jax import lax
from jax.experimental import pallas as pl
from jax.experimental.pallas import tpu as pltpu
from jax.sharding import PartitionSpec as P

L = 512
D = 1024
TIMES = 32
LOG2E = 1.4426950408889634
BF = jnp.bfloat16
F32 = jnp.float32
MESH = pl.DeviceIdType.MESH

ORDERS = (("x", "y", "z"), ("y", "z", "x"), ("z", "x", "y"))
A, G1, G2, D1, D2 = range(5)
BATCHES = (
    ((("q", 0, 64),), (("k", 0, 64),), (("v", 0, 64),)),
    (
        (("o", 0, 32), ("g0", 0, 64)),
        (("o", 32, 16), ("u0", 0, 64)),
        (("o", 48, 16), ("g1", 0, 64)),
    ),
    ((("u1", 0, 64),), (("g2", 0, 64),), (("u2", 0, 64),)),
    ((("d0", 0, 48),), (("d0", 48, 16), ("d1", 0, 32)), (("d1", 32, 32),)),
    ((("d2", 0, 16),), (("d2", 16, 16),), (("d2", 32, 32),)),
)
ROWS = tuple(tuple(sum(p[2] for p in pieces) for pieces in batch) for batch in BATCHES)
HALF = tuple(tuple((r // 16 + 1) // 2 * 16 for r in rows) for rows in ROWS)
OWN = 24
NS = 25
VMEM = 58 * 2**20


def whereabouts(name):
    found = []
    for b, batch in enumerate(BATCHES):
        for c, pieces in enumerate(batch):
            row = 0
            for piece, first, count in pieces:
                if piece == name:
                    found.append((first, b, c, row, count))
                row += count
    return [part[1:] for part in sorted(found)]


class Exchange:
    def __init__(self, bufs, send, recv):
        self.bufs, self.send, self.recv = bufs, send, recv
        dp, mp = lax.axis_index("dp"), lax.axis_index("mp")
        self.pos = {"x": lax.rem(dp, 4), "y": dp // 4, "z": mp // 2}
        self.core = lax.rem(mp, 2)
        self.started = []

    def device(self, axis=None, step=0):
        pos = dict(self.pos)
        core = self.core
        if axis == "core":
            core = 1 - core
        elif axis is not None:
            pos[axis] = lax.rem(pos[axis] + step + 4, 4)
        return (pos["y"] * 4 + pos["x"], pos["z"] * 2 + core)

    def slab(self, b, c, phase, shift, half):
        a1, a2, a3 = ORDERS[c]
        at = {k: self.pos[k] for k in "xyz"}
        axis = ORDERS[c][phase]
        at[axis] = lax.rem(at[axis] + shift + 4, 4)
        buf = self.bufs[b][c]
        base = self.core * 64 + at[a3] * 16
        if phase == 0:
            first = base + at[a2] * 4 + at[a1]
            top = HALF[b][c]
            rows = pl.ds(0, top) if half == 0 else pl.ds(top, ROWS[b][c] - top)
            return buf.at[pl.ds(first, 1), rows]
        if phase == 1:
            return buf.at[pl.ds(base + at[a2] * 4 + 2 * half, 2)]
        return buf.at[pl.ds(base + 8 * half, 8)]

    def copy(self, ref, b, c, slot, device):
        return pltpu.make_async_remote_copy(
            src_ref=ref,
            dst_ref=ref,
            send_sem=self.send.at[b, c, slot],
            recv_sem=self.recv.at[b, c, slot],
            device_id=device,
            device_id_type=MESH,
        )

    def start(self, b, c, slot, ref, device):
        copy = self.copy(ref, b, c, slot, device)
        copy.start()
        self.started.append(copy)

    def first(self, b, c, p):
        axis = ORDERS[c][p]
        for slot, half, step in ((0, 0, 1), (2, 1, -1), (1, 1, 1), (3, 0, -1)):
            if self.empty(b, c, p, half):
                continue
            self.start(b, c, p * 6 + slot, self.slab(b, c, p, 0, half), self.device(axis, step))

    def empty(self, b, c, p, half):
        return p == 0 and half == 1 and HALF[b][c] == ROWS[b][c]

    def landed(self, b, c, p, slot):
        half = (0, 1, 1, 0, 0, 1)[slot]
        shift = (-1, -1, 1, 1, -2, 2)[slot]
        ref = self.slab(b, c, p, shift, half)
        self.copy(ref, b, c, p * 6 + slot, self.device(ORDERS[c][p], 1)).wait_recv()
        return ref

    def forward(self, b, c, p):
        axis = ORDERS[c][p]
        for slot, step in ((0, 1), (2, -1)):
            if self.empty(b, c, p, slot // 2):
                continue
            ref = self.landed(b, c, p, slot)
            self.start(b, c, p * 6 + 4 + slot // 2, ref, self.device(axis, step))
            if p == 2:
                self.share(b, c, slot, ref)

    def finish(self, b, c, p, slots=(1, 3, 4, 5)):
        for slot in slots:
            if self.empty(b, c, p, (0, 1, 1, 0, 0, 1)[slot]):
                continue
            ref = self.landed(b, c, p, slot)
            if p == 2:
                self.share(b, c, slot, ref)

    def share(self, b, c, slot, ref):
        self.start(b, c, 18 + slot, ref, self.device("core"))

    def plane(self, b, c, core):
        return self.bufs[b][c].at[pl.ds(core * 64 + self.pos[ORDERS[c][2]] * 16, 16)]

    def share_own(self, b, c):
        self.start(b, c, OWN, self.plane(b, c, self.core), self.device("core"))

    def shared(self, b, c):
        other = self.device("core")
        self.copy(self.plane(b, c, self.core), b, c, OWN, other).wait_recv()
        for slot in range(6):
            ref = self.slab(b, c, 2, (-1, -1, 1, 1, -2, 2)[slot], (0, 1, 1, 0, 0, 1)[slot])
            self.copy(ref, b, c, 18 + slot, other).wait_recv()

    def every(self, action, p, *batches):
        for b in batches:
            for c in range(3):
                action(b, c, p)

    def finish_some(self, b, slots):
        for c in range(3):
            self.finish(b, c, 2, slots)

    def own_planes(self, *batches):
        for b in batches:
            for c in range(3):
                self.share_own(b, c)

    def complete(self, b):
        for c in range(3):
            self.shared(b, c)


def nt(a, b):
    return lax.dot_general(a, b, (((1,), (1,)), ((), ())), preferred_element_type=F32)


def nn(a, b):
    return jnp.dot(a, b, preferred_element_type=F32)


def spot(c, core, x, y, z):
    at = {"x": x, "y": y, "z": z}
    a1, a2, a3 = ORDERS[c]
    return core * 64 + at[a3] * 16 + at[a2] * 4 + at[a1]


def normed_into(dst, src, gain, row):
    g = gain[pl.ds(row, 1), :]

    def block(i, _):
        rows = pl.ds(pl.multiple_of(i * 64, 64), 64)
        wide = src[rows, :].astype(F32)
        square = jnp.mean(wide * wide, axis=-1, keepdims=True)
        dst[rows, :] = (wide * lax.rsqrt(square + 1e-05) * g).astype(BF)
        return 0

    lax.fori_loop(0, 8, block, 0)


def kernel(
    tok_hbm, gain, qkvw, outw, ffnw, downw, table, bias, sids, vids, tids,
    out, *scratch,
):
    chunks = scratch[:15]
    (tok, xn, same, away, cq, sq, ck, sk, qs, ks, vs, att, res, hid, half, acc,
     stage, tok_sem, send, recv) = scratch[15:]
    ex = Exchange([chunks[3 * b : 3 * b + 3] for b in range(5)], send, recv)

    def tile_of(name):
        if name in "qkv":
            return qkvw.at["qkv".index(name)]
        if name == "o":
            return outw
        lanes = pl.ds(int(name[1]) * 128, 128)
        return downw.at[:, lanes] if name[0] == "d" else ffnw.at["gu".index(name[0]), :, lanes]

    def owns(b):
        copies = []
        for c, pieces in enumerate(BATCHES[b]):
            at = ex.bufs[b][c].at[spot(c, ex.core, ex.pos["x"], ex.pos["y"], ex.pos["z"])]
            row = 0
            for k, (name, first, count) in enumerate(pieces):
                copies.append(
                    pltpu.make_async_copy(
                        tile_of(name).at[pl.ds(first, count)],
                        at.at[pl.ds(row, count)],
                        stage.at[b, c, k],
                    )
                )
                row += count
        return copies

    for b in range(5):
        for copy in owns(b):
            copy.start()
    fetch = pltpu.make_async_copy(tok_hbm, tok, tok_sem)
    fetch.start()
    barrier = pltpu.get_barrier_semaphore()
    for axis in "xyz":
        for step in (1, -1):
            pl.semaphore_signal(barrier, inc=1, device_id=ex.device(axis, step), device_id_type=MESH)
    pl.semaphore_signal(barrier, inc=1, device_id=ex.device("core"), device_id_type=MESH)
    pl.semaphore_wait(barrier, 7)

    for b in range(5):
        for copy in owns(b):
            copy.wait()
        ex.every(ex.first, 0, b)

    eye = (
        lax.broadcasted_iota(jnp.int32, (L, L), 0) == lax.broadcasted_iota(jnp.int32, (L, L), 1)
    ).astype(F32).astype(BF)

    def column(ids):
        row = jnp.broadcast_to(ids[...].astype(F32), (128, L)).astype(BF)
        return nt(eye, row)

    def matches(ids):
        col = column(ids)
        row = jnp.broadcast_to(ids[...].astype(F32), (L, L))
        return jnp.concatenate([col] * 4, axis=1) == row

    same[...] = jnp.where(matches(vids), 1.0, 0.0)
    away[...] = jnp.where(matches(sids), 0.0, -1e30)

    ex.every(ex.forward, 0, A, G1, G2, D1, D2)
    fetch.wait()
    normed_into(xn, tok, gain, 0)
    for b in (A, G1, G2):
        ex.every(ex.finish, 0, b)
        ex.every(ex.first, 1, b)
    ex.every(ex.finish, 0, D1, D2)

    lanes = lax.broadcasted_iota(jnp.int32, (L, 128), 1).astype(F32)
    hot = jnp.where(column(tids) == lanes, 1.0, 0.0).astype(BF)
    turn = nn(hot, table[...])
    cos = turn[:, 0:128] + turn[:, 256:384] + turn[:, 512:640]
    sin = turn[:, 128:256] + turn[:, 384:512] + turn[:, 640:768]
    cq[...] = cos * (LOG2E / 8.0)
    sq[...] = sin * (LOG2E / 8.0)
    ck[...] = cos
    sk[...] = sin

    ex.every(ex.forward, 1, A)
    ex.every(ex.first, 1, D1, D2)
    ex.every(ex.forward, 1, G1)
    ex.every(ex.finish, 1, A)
    ex.every(ex.first, 2, A)
    ex.own_planes(A)
    ex.every(ex.forward, 1, G2, D1, D2)
    ex.every(ex.finish, 1, G1)
    ex.own_planes(G1)
    ex.every(ex.forward, 2, A)
    ex.every(ex.first, 2, G1)
    ex.finish_some(A, (1, 3))
    ex.every(ex.finish, 1, G2, D1, D2)
    ex.finish_some(A, (4, 5))
    ex.own_planes(G2, D1, D2)
    ex.complete(A)

    def columns(name, z):
        sides = []
        for core in range(2):
            parts = [
                ex.bufs[b][c][spot(c, core, x, y, z), pl.ds(row, count), :]
                for y in range(4)
                for x in range(4)
                for b, c, row, count in whereabouts(name)
            ]
            sides.append(jnp.concatenate(parts, axis=0))
        return jnp.concatenate(sides, axis=1)

    def outputs(names, y):
        wide = []
        for z in range(4):
            for name in names:
                for core in range(2):
                    parts = [
                        ex.bufs[b][c][spot(c, core, x, y, z), pl.ds(row, count), :]
                        for x in range(4)
                        for b, c, row, count in whereabouts(name)
                    ]
                    wide.append(jnp.concatenate(parts, axis=0))
        return jnp.concatenate(wide, axis=1)

    def turned(raw, cosine, sine):
        lane = lax.rem(lax.broadcasted_iota(jnp.int32, (L, 128), 1), 64)
        done = []
        for t in range(2):
            v = raw[:, t * 128 : (t + 1) * 128]
            other = jnp.where(lane < 32, pltpu.roll(v, 96, 1), pltpu.roll(v, 32, 1))
            done.append(v * cosine[...] + other * sine[...])
        return jnp.concatenate(done, axis=1).astype(BF)

    def group(z):
        qs[...] = turned(nn(xn[...], columns("q", z)), cq, sq)
        ks[...] = turned(nn(xn[...], columns("k", z)), ck, sk)
        vs[...] = nn(xn[...], columns("v", z)).astype(BF)

        def head(h):
            mine = lax.broadcasted_iota(jnp.int32, (L, 256), 1) // 64 == h
            q = jnp.where(mine, qs[...], jnp.zeros((), BF))
            s = nt(q, ks[...]) + same[...] * ((bias[0, z * 4 + h] - bias[1, z * 4 + h]) * LOG2E) + away[...]
            e = jnp.exp2(s - jnp.max(s, axis=1, keepdims=True))
            total = jnp.sum(e, axis=1, keepdims=True)
            got = (nn(e.astype(BF), vs[...]) * (1.0 / total)).astype(BF)
            here = pl.ds(z * 256, 256)
            att[:, here] = jnp.where(mine, got, att[:, here])

        for h in range(4):
            head(h)

    att[...] = jnp.zeros_like(att)
    group(0)
    ex.every(ex.forward, 2, G1)
    ex.every(ex.first, 2, G2)
    group(1)
    group(2)
    ex.finish_some(G1, (1, 3))
    group(3)
    ex.finish_some(G1, (4, 5))
    ex.every(ex.forward, 2, G2)
    ex.every(ex.first, 2, D1, D2)
    ex.complete(G1)

    def here(y):
        return pl.ds(pl.multiple_of(y * 256, 256), 256)

    def project(y, _):
        mixed = nt(att[...], outputs(("o",), y))
        res[:, here(y)] = (tok[:, here(y)].astype(F32) + mixed).astype(BF)
        return 0

    lax.fori_loop(0, 4, project, 0)
    normed_into(xn, res, gain, 1)

    def soft(gate):
        return gate / (1.0 + jnp.exp(-gate))

    def feed(k, gate, up):
        def step(z, _):
            bent = half[:, here(z)] if gate is None else soft(nn(xn[...], columns(gate, z)))
            hidden = bent * nn(xn[...], columns(up, z))
            hid[:, pl.ds(pl.multiple_of(k * 1024 + z * 256, 256), 256)] = hidden.astype(BF)
            return 0

        lax.fori_loop(0, 4, step, 0)

    def gates(z, _):
        half[:, here(z)] = soft(nn(xn[...], columns("g1", z)))
        return 0

    feed(0, "g0", "u0")
    ex.finish_some(G2, (1, 3, 4, 5))
    lax.fori_loop(0, 4, gates, 0)
    ex.every(ex.forward, 2, D1, D2)
    ex.complete(G2)
    feed(1, None, "u1")
    ex.finish_some(D1, (1, 3))
    feed(2, "g2", "u2")
    ex.finish_some(D1, (4, 5))
    ex.every(ex.finish, 2, D2)
    ex.complete(D1)

    def down_first(y, _):
        at = pl.ds(0, 2048)
        wide = [outputs((name,), y) for name in ("d0", "d1")]
        acc[:, here(y)] = res[:, here(y)].astype(F32) + nt(
            hid[:, at], jnp.concatenate(wide, axis=1)
        )
        return 0

    def down_last(y, _):
        fed = nt(hid[:, pl.ds(2048, 1024)], outputs(("d2",), y))
        out[:, here(y)] = (acc[:, here(y)] + fed).astype(BF)
        return 0

    lax.fori_loop(0, 4, down_first, 0)
    ex.complete(D2)
    lax.fori_loop(0, 4, down_last, 0)
    for copy in ex.started:
        copy.wait_send()


def turn_table():
    freq = 10000.0 ** (-np.arange(32) / 32.0)
    angle = np.arange(TIMES)[:, None] * freq[None, :]
    cos = np.tile(np.cos(angle), (1, 4))
    sin = np.sin(angle)
    sin = np.tile(np.concatenate([-sin, sin], axis=1), (1, 2))
    left = np.concatenate([cos, sin], axis=1).astype(np.float32)
    terms = []
    for _ in range(3):
        term = left.astype(BF)
        terms.append(term)
        left = left - term.astype(np.float32)
    rows = np.concatenate(terms, axis=1)
    return np.concatenate([rows, np.zeros((128 - TIMES, rows.shape[1]), BF)], axis=0)


def local(
    tokens,
    norm_gain,
    qkv_weight,
    out_weight,
    variate_bias,
    ffn_weight,
    down_weight,
    sample_ids,
    variate_ids,
    time_ids,
):
    ffn_wide = jnp.pad(ffn_weight, ((0, 0), (0, 0), (0, 32)))
    down_wide = jnp.pad(down_weight.T, ((0, 0), (0, 32)))
    vmem = pl.BlockSpec(memory_space=pltpu.VMEM)
    hbm = pl.BlockSpec(memory_space=pl.ANY)
    smem = pl.BlockSpec(memory_space=pltpu.SMEM)
    buffers = [
        pltpu.VMEM((128, ROWS[b][c], 128), BF) for b in range(5) for c in range(3)
    ]
    return pl.pallas_call(
        kernel,
        out_shape=jax.ShapeDtypeStruct((L, D), BF),
        in_specs=[hbm, vmem, hbm, hbm, hbm, hbm, vmem, smem, vmem, vmem, vmem],
        out_specs=vmem,
        scratch_shapes=buffers
        + [
            pltpu.VMEM((L, D), BF),
            pltpu.VMEM((L, D), BF),
            pltpu.VMEM((L, L), F32),
            pltpu.VMEM((L, L), F32),
            pltpu.VMEM((L, 128), F32),
            pltpu.VMEM((L, 128), F32),
            pltpu.VMEM((L, 128), F32),
            pltpu.VMEM((L, 128), F32),
            pltpu.VMEM((L, 256), BF),
            pltpu.VMEM((L, 256), BF),
            pltpu.VMEM((L, 256), BF),
            pltpu.VMEM((L, D), BF),
            pltpu.VMEM((L, D), BF),
            pltpu.VMEM((L, 3072), BF),
            pltpu.VMEM((L, D), F32),
            pltpu.VMEM((L, D), F32),
            pltpu.SemaphoreType.DMA((5, 3, 2)),
            pltpu.SemaphoreType.DMA,
            pltpu.SemaphoreType.DMA((5, 3, NS)),
            pltpu.SemaphoreType.DMA((5, 3, NS)),
        ],
        compiler_params=pltpu.CompilerParams(
            collective_id=0, has_side_effects=True, vmem_limit_bytes=VMEM
        ),
    )(
        tokens,
        norm_gain,
        qkv_weight,
        out_weight.T,
        ffn_wide,
        down_wide,
        jnp.asarray(turn_table()),
        variate_bias,
        sample_ids.reshape(1, L),
        variate_ids.reshape(1, L),
        time_ids.reshape(1, L),
    )


def solution(mesh):
    return jax.shard_map(
        local,
        mesh=mesh,
        in_specs=(
            P(("dp", "mp"), None),
            P(),
            P(None, "dp", "mp"),
            P("mp", "dp"),
            P(),
            P(None, "dp", "mp"),
            P("mp", "dp"),
            P(("dp", "mp")),
            P(("dp", "mp")),
            P(("dp", "mp")),
        ),
        out_specs=P(("dp", "mp"), None),
        check_vma=False,
    )
```

time: 109 us -> 85.8 us (0.79)
  Pallas kernels: 97.7 us -> 81.3 us
  local copies, waits for them, and re-layouts: 9.95 us -> 4.38 us
  other arithmetic: 1.34 us -> 0 us
    pallas_call x1, Pallas kernels: 97.7 us -> 81.3 us  [local(): pl.pallas_call(kernel, out_shape=jax.ShapeDtypeStruct((L, D), BF), in_spe...]
    unnamed x13 -> x3, local copies, waits for them, and re-layouts: 7.9 us -> 2.27 us
    pad x0 -> x2, local copies, waits for them, and re-layouts: none -> 2.11 us  [the longest x1 1.45 us: local(): down_wide = jnp.pad(down_weight.T, ((0, 0), (0, 32)))]
    transpose x1 -> x0, local copies, waits for them, and re-layouts: 1.44 us -> none  [local(): packc = tall.reshape(64, 3, 128).transpose(1, 0, 2)]
    mul x1 -> x0, other arithmetic: 1.34 us -> none  [local(): slope = (variate_bias[0] - variate_bias[1]) * LOG2E]
where the time goes in v1:
time: 85.8 us; the launch traced here: 85.7 us
  Pallas kernels  81.3 us (95%)
  local copies, waits for them, and re-layouts  4.38 us (5%)
    pallas_call x1, Pallas kernels, local(): pl.pallas_call(kernel, out_shape=jax.ShapeDtypeStruct((L, D), BF), in_spe...  81.3 us
    unnamed x3, local copies, waits for them, and re-layouts  2.27 us

profile of v1, /device:TPU:1, one launch (start us, length us, event | category | flops | bytes accessed | tf_op | source)
XLA Modules:
  0.0 85.7 jit_solution(17507143183977307926)
XLA Ops:
  0.0 0.0 copy-start
  0.0 1.5 %pad.9.downw = bf16[64,384]{1,0:T(8,128)(2,1)} pad(bf16[64,352]{1,0:T(8,128)(2,1)} %bitcast.5, bf16[]{:T(256)} %constant.4.clone.1), padding=0_0x0_32 | pad | bytes 94210 | tf_op jit(solution)/shard_map/jit(_pad)/pad | solution.py:448
  1.5 0.0 copy-done
  1.5 0.7 pad.8.ffnw
  2.1 81.3 %shard_map.109 = bf16[512,1024]{1,0:T(8,128)(2,1)} custom-call(bf16[512,1024]{1,0:T(8,128)(2,1)} %tok_hbm.1, f32[2,1024]{1,0:T(2,128)} %gain.1, bf16[3,64,128]{2,1,0:T(8,128)(2,1)} %qkvw.1, bf16[64,128]{1,0:T(8,128)(2,1)} %bitcast.6, bf16[2,64,384]{2,1,0:T(8,128)(2,1)} %pad.8.ffnw, bf16[64,384]{1,0:T(8,128)(2,1)} %pad.9.downw, ...), custom_call_target="tpu_custom_call" | custom-call | tf_op jit(solution)/shard_map/pallas_call | solution.py:455
  83.4 2.3 %copy.13 = bf16[512,1024]{1,0:T(8,128)(2,1)} copy(bf16[512,1024]{1,0:T(8,128)(2,1)} %shard_map.109) | data formatting | bytes 2097152
Async XLA Ops:
  0.0 1.5 %copy-start = (bf16[2,64,352]{2,1,0:T(8,128)(2,1)S(1)}, bf16[2,64,352]{2,1,0:T(8,128)(2,1)}, u32[]{:S(2)}) copy-start(bf16[2,64,352]{2,1,0:T(8,128)(2,1)} %param.16) | copy-start | bytes 270340

commit v2 on v1

--- a/solution.py
+++ b/solution.py
@@ -28,9 +28,16 @@
     ((("d2", 0, 16),), (("d2", 16, 16),), (("d2", 32, 32),)),
 )
 ROWS = tuple(tuple(sum(p[2] for p in pieces) for pieces in batch) for batch in BATCHES)
-HALF = tuple(tuple((r // 16 + 1) // 2 * 16 for r in rows) for rows in ROWS)
-OWN = 24
-NS = 25
+START = tuple(tuple(sum(ROWS[k][c] for k in range(b)) for c in range(3)) for b in range(6))
+GROUPS = (
+    ((A, G1), (G1, D2 + 1)),
+    ((A, G1), (G1, G2), (G2, D2 + 1)),
+    tuple((b, b + 1) for b in range(5)),
+)
+FIRST_SEM = (0, 36, 90, 180, 270)
+SEMS = 276
+HALF_OF = (0, 1, 1, 0, 0, 1)
+SHIFT_OF = (-1, -1, 1, 1, -2, 2)
 VMEM = 58 * 2**20
 
 
@@ -41,7 +48,7 @@
             row = 0
             for piece, first, count in pieces:
                 if piece == name:
-                    found.append((first, b, c, row, count))
+                    found.append((first, c, START[b][c] + row, count))
                 row += count
     return [part[1:] for part in sorted(found)]
 
@@ -63,105 +70,104 @@
             pos[axis] = lax.rem(pos[axis] + step + 4, 4)
         return (pos["y"] * 4 + pos["x"], pos["z"] * 2 + core)
 
-    def slab(self, b, c, phase, shift, half):
+    def span(self, p, g, c):
+        first, last = GROUPS[p][g]
+        return START[first][c], START[last][c]
+
+    def slab(self, p, g, c, shift, half):
         a1, a2, a3 = ORDERS[c]
         at = {k: self.pos[k] for k in "xyz"}
-        axis = ORDERS[c][phase]
+        axis = ORDERS[c][p]
         at[axis] = lax.rem(at[axis] + shift + 4, 4)
-        buf = self.bufs[b][c]
+        low, high = self.span(p, g, c)
         base = self.core * 64 + at[a3] * 16
-        if phase == 0:
-            first = base + at[a2] * 4 + at[a1]
-            top = HALF[b][c]
-            rows = pl.ds(0, top) if half == 0 else pl.ds(top, ROWS[b][c] - top)
-            return buf.at[pl.ds(first, 1), rows]
-        if phase == 1:
-            return buf.at[pl.ds(base + at[a2] * 4 + 2 * half, 2)]
-        return buf.at[pl.ds(base + 8 * half, 8)]
-
-    def copy(self, ref, b, c, slot, device):
+        count = (1, 4, 16)[p]
+        if p < 2:
+            base = base + at[a2] * 4
+        if p < 1:
+            base = base + at[a1]
+        if half is not None and p == 0:
+            middle = low + ((high - low) // 16 + 1) // 2 * 16
+            low, high = ((low, middle), (middle, high))[half]
+        elif half is not None:
+            count = count // 2
+            base = base + half * count
+        return self.bufs[c].at[pl.ds(base, count), pl.ds(low, high - low)]
+
+    def copy(self, ref, sem, device):
         return pltpu.make_async_remote_copy(
             src_ref=ref,
             dst_ref=ref,
-            send_sem=self.send.at[b, c, slot],
-            recv_sem=self.recv.at[b, c, slot],
+            send_sem=self.send.at[sem],
+            recv_sem=self.recv.at[sem],
             device_id=device,
             device_id_type=MESH,
         )
 
-    def start(self, b, c, slot, ref, device):
-        copy = self.copy(ref, b, c, slot, device)
+    def start(self, ref, sem, device):
+        copy = self.copy(ref, sem, device)
         copy.start()
         self.started.append(copy)
 
-    def first(self, b, c, p):
-        axis = ORDERS[c][p]
-        for slot, half, step in ((0, 0, 1), (2, 1, -1), (1, 1, 1), (3, 0, -1)):
-            if self.empty(b, c, p, half):
-                continue
-            self.start(b, c, p * 6 + slot, self.slab(b, c, p, 0, half), self.device(axis, step))
-
-    def empty(self, b, c, p, half):
-        return p == 0 and half == 1 and HALF[b][c] == ROWS[b][c]
-
-    def landed(self, b, c, p, slot):
-        half = (0, 1, 1, 0, 0, 1)[slot]
-        shift = (-1, -1, 1, 1, -2, 2)[slot]
-        ref = self.slab(b, c, p, shift, half)
-        self.copy(ref, b, c, p * 6 + slot, self.device(ORDERS[c][p], 1)).wait_recv()
+    def sem(self, p, g, c, slot):
+        return FIRST_SEM[p] + (g * 3 + c) * 6 + slot
+
+    def first(self, p, g):
+        for c in range(3):
+            axis = ORDERS[c][p]
+            for slot, step in ((0, 1), (2, -1), (1, 1), (3, -1)):
+                if p == 0 and slot % 2:
+                    continue
+                half = None if p == 0 else HALF_OF[slot]
+                self.start(
+                    self.slab(p, g, c, 0, half), self.sem(p, g, c, slot), self.device(axis, step)
+                )
+
+    def landed(self, p, g, c, slot):
+        half = None if p == 0 and slot < 4 else HALF_OF[slot]
+        ref = self.slab(p, g, c, SHIFT_OF[slot], half)
+        self.copy(ref, self.sem(p, g, c, slot), self.device(ORDERS[c][p], 1)).wait_recv()
         return ref
 
-    def forward(self, b, c, p):
-        axis = ORDERS[c][p]
-        for slot, step in ((0, 1), (2, -1)):
-            if self.empty(b, c, p, slot // 2):
-                continue
-            ref = self.landed(b, c, p, slot)
-            self.start(b, c, p * 6 + 4 + slot // 2, ref, self.device(axis, step))
-            if p == 2:
-                self.share(b, c, slot, ref)
-
-    def finish(self, b, c, p, slots=(1, 3, 4, 5)):
-        for slot in slots:
-            if self.empty(b, c, p, (0, 1, 1, 0, 0, 1)[slot]):
-                continue
-            ref = self.landed(b, c, p, slot)
-            if p == 2:
-                self.share(b, c, slot, ref)
-
-    def share(self, b, c, slot, ref):
-        self.start(b, c, 18 + slot, ref, self.device("core"))
-
-    def plane(self, b, c, core):
-        return self.bufs[b][c].at[pl.ds(core * 64 + self.pos[ORDERS[c][2]] * 16, 16)]
-
-    def share_own(self, b, c):
-        self.start(b, c, OWN, self.plane(b, c, self.core), self.device("core"))
-
-    def shared(self, b, c):
+    def forward(self, p, g):
+        for c in range(3):
+            axis = ORDERS[c][p]
+            for slot, step in ((0, 1), (2, -1)):
+                self.landed(p, g, c, slot)
+                ref = self.slab(p, g, c, SHIFT_OF[slot], HALF_OF[slot])
+                self.start(ref, self.sem(p, g, c, 4 + slot // 2), self.device(axis, step))
+                if p == 2:
+                    self.share(g, c, slot, ref)
+
+    def finish(self, p, g, slots=(1, 3, 4, 5)):
+        for c in range(3):
+            for slot in slots:
+                if p == 0 and slot < 4:
+                    continue
+                ref = self.landed(p, g, c, slot)
+                if p == 2:
+                    self.share(g, c, slot, ref)
+
+    def share(self, g, c, slot, ref):
+        self.start(ref, self.sem(3, g, c, slot), self.device("core"))
+
+    def plane(self, k, c):
+        low, high = self.span(0, k, c)
+        first = self.core * 64 + self.pos[ORDERS[c][2]] * 16
+        return self.bufs[c].at[pl.ds(first, 16), pl.ds(low, high - low)]
+
+    def share_own(self, k):
+        for c in range(3):
+            self.start(self.plane(k, c), FIRST_SEM[4] + k * 3 + c, self.device("core"))
+
+    def complete(self, g):
         other = self.device("core")
-        self.copy(self.plane(b, c, self.core), b, c, OWN, other).wait_recv()
-        for slot in range(6):
-            ref = self.slab(b, c, 2, (-1, -1, 1, 1, -2, 2)[slot], (0, 1, 1, 0, 0, 1)[slot])
-            self.copy(ref, b, c, 18 + slot, other).wait_recv()
-
-    def every(self, action, p, *batches):
-        for b in batches:
-            for c in range(3):
-                action(b, c, p)
-
-    def finish_some(self, b, slots):
         for c in range(3):
-            self.finish(b, c, 2, slots)
-
-    def own_planes(self, *batches):
-        for b in batches:
-            for c in range(3):
-                self.share_own(b, c)
-
-    def complete(self, b):
-        for c in range(3):
-            self.shared(b, c)
+            if g < 2:
+                self.copy(self.plane(g, c), FIRST_SEM[4] + g * 3 + c, other).wait_recv()
+            for slot in range(6):
+                ref = self.slab(2, g, c, SHIFT_OF[slot], HALF_OF[slot])
+                self.copy(ref, self.sem(3, g, c, slot), other).wait_recv()
 
 
 def nt(a, b):
@@ -192,13 +198,12 @@
 
 
 def kernel(
-    tok_hbm, gain, qkvw, outw, ffnw, downw, table, bias, sids, vids, tids,
+    tok_hbm, gain, qkvw, outw, wide, table, bias, sids, vids, tids,
     out, *scratch,
 ):
-    chunks = scratch[:15]
     (tok, xn, same, away, cq, sq, ck, sk, qs, ks, vs, att, res, hid, half, acc,
-     stage, tok_sem, send, recv) = scratch[15:]
-    ex = Exchange([chunks[3 * b : 3 * b + 3] for b in range(5)], send, recv)
+     stage, tok_sem, send, recv) = scratch[3:]
+    ex = Exchange(scratch[:3], send, recv)
 
     def tile_of(name):
         if name in "qkv":
@@ -206,13 +211,13 @@
         if name == "o":
             return outw
         lanes = pl.ds(int(name[1]) * 128, 128)
-        return downw.at[:, lanes] if name[0] == "d" else ffnw.at["gu".index(name[0]), :, lanes]
+        return wide.at["gud".index(name[0]), :, lanes]
 
     def owns(b):
         copies = []
         for c, pieces in enumerate(BATCHES[b]):
-            at = ex.bufs[b][c].at[spot(c, ex.core, ex.pos["x"], ex.pos["y"], ex.pos["z"])]
-            row = 0
+            at = ex.bufs[c].at[spot(c, ex.core, ex.pos["x"], ex.pos["y"], ex.pos["z"])]
+            row = START[b][c]
             for k, (name, first, count) in enumerate(pieces):
                 copies.append(
                     pltpu.make_async_copy(
@@ -236,10 +241,11 @@
     pl.semaphore_signal(barrier, inc=1, device_id=ex.device("core"), device_id_type=MESH)
     pl.semaphore_wait(barrier, 7)
 
-    for b in range(5):
-        for copy in owns(b):
-            copy.wait()
-        ex.every(ex.first, 0, b)
+    for k in range(2):
+        for b in range(*GROUPS[0][k]):
+            for copy in owns(b):
+                copy.wait()
+        ex.first(0, k)
 
     eye = (
         lax.broadcasted_iota(jnp.int32, (L, L), 0) == lax.broadcasted_iota(jnp.int32, (L, L), 1)
@@ -257,13 +263,13 @@
     same[...] = jnp.where(matches(vids), 1.0, 0.0)
     away[...] = jnp.where(matches(sids), 0.0, -1e30)
 
-    ex.every(ex.forward, 0, A, G1, G2, D1, D2)
+    ex.forward(0, 0)
+    ex.forward(0, 1)
     fetch.wait()
     normed_into(xn, tok, gain, 0)
-    for b in (A, G1, G2):
-        ex.every(ex.finish, 0, b)
-        ex.every(ex.first, 1, b)
-    ex.every(ex.finish, 0, D1, D2)
+    for k in range(2):
+        ex.finish(0, k)
+        ex.first(1, k)
 
     lanes = lax.broadcasted_iota(jnp.int32, (L, 128), 1).astype(F32)
     hot = jnp.where(column(tids) == lanes, 1.0, 0.0).astype(BF)
@@ -275,31 +281,30 @@
     ck[...] = cos
     sk[...] = sin
 
-    ex.every(ex.forward, 1, A)
-    ex.every(ex.first, 1, D1, D2)
-    ex.every(ex.forward, 1, G1)
-    ex.every(ex.finish, 1, A)
-    ex.every(ex.first, 2, A)
-    ex.own_planes(A)
-    ex.every(ex.forward, 1, G2, D1, D2)
-    ex.every(ex.finish, 1, G1)
-    ex.own_planes(G1)
-    ex.every(ex.forward, 2, A)
-    ex.every(ex.first, 2, G1)
-    ex.finish_some(A, (1, 3))
-    ex.every(ex.finish, 1, G2, D1, D2)
-    ex.finish_some(A, (4, 5))
-    ex.own_planes(G2, D1, D2)
+    ex.forward(1, 0)
+    ex.first(1, 2)
+    ex.forward(1, 1)
+    ex.finish(1, 0)
+    ex.first(2, A)
+    ex.share_own(0)
+    ex.forward(1, 2)
+    ex.finish(1, 1)
+    ex.forward(2, A)
+    ex.first(2, G1)
+    ex.finish(2, A, (1, 3))
+    ex.finish(1, 2)
+    ex.finish(2, A, (4, 5))
+    ex.share_own(1)
     ex.complete(A)
 
     def columns(name, z):
         sides = []
         for core in range(2):
             parts = [
-                ex.bufs[b][c][spot(c, core, x, y, z), pl.ds(row, count), :]
+                ex.bufs[c][spot(c, core, x, y, z), pl.ds(row, count), :]
                 for y in range(4)
                 for x in range(4)
-                for b, c, row, count in whereabouts(name)
+                for c, row, count in whereabouts(name)
             ]
             sides.append(jnp.concatenate(parts, axis=0))
         return jnp.concatenate(sides, axis=1)
@@ -310,9 +315,9 @@
             for name in names:
                 for core in range(2):
                     parts = [
-                        ex.bufs[b][c][spot(c, core, x, y, z), pl.ds(row, count), :]
+                        ex.bufs[c][spot(c, core, x, y, z), pl.ds(row, count), :]
                         for x in range(4)
-                        for b, c, row, count in whereabouts(name)
+                        for c, row, count in whereabouts(name)
                     ]
                     wide.append(jnp.concatenate(parts, axis=0))
         return jnp.concatenate(wide, axis=1)
@@ -326,7 +331,7 @@
             done.append(v * cosine[...] + other * sine[...])
         return jnp.concatenate(done, axis=1).astype(BF)
 
-    def group(z):
+    def group(z, between=None, at=0):
         qs[...] = turned(nn(xn[...], columns("q", z)), cq, sq)
         ks[...] = turned(nn(xn[...], columns("k", z)), ck, sk)
         vs[...] = nn(xn[...], columns("v", z)).astype(BF)
@@ -342,19 +347,17 @@
             att[:, here] = jnp.where(mine, got, att[:, here])
 
         for h in range(4):
+            if between is not None and h == at:
+                between()
             head(h)
 
     att[...] = jnp.zeros_like(att)
-    group(0)
-    ex.every(ex.forward, 2, G1)
-    ex.every(ex.first, 2, G2)
+    group(0, lambda: (ex.forward(2, G1), ex.first(2, G2)))
     group(1)
+    ex.finish(2, G1, (1, 3))
     group(2)
-    ex.finish_some(G1, (1, 3))
-    group(3)
-    ex.finish_some(G1, (4, 5))
-    ex.every(ex.forward, 2, G2)
-    ex.every(ex.first, 2, D1, D2)
+    ex.finish(2, G1, (4, 5))
+    group(3, lambda: (ex.forward(2, G2), ex.first(2, D1), ex.first(2, D2)), 2)
     ex.complete(G1)
 
     def here(y):
@@ -385,15 +388,15 @@
         return 0
 
     feed(0, "g0", "u0")
-    ex.finish_some(G2, (1, 3, 4, 5))
+    ex.finish(2, G2)
+    ex.forward(2, D1)
     lax.fori_loop(0, 4, gates, 0)
-    ex.every(ex.forward, 2, D1, D2)
     ex.complete(G2)
+    ex.forward(2, D2)
     feed(1, None, "u1")
-    ex.finish_some(D1, (1, 3))
+    ex.finish(2, D1)
     feed(2, "g2", "u2")
-    ex.finish_some(D1, (4, 5))
-    ex.every(ex.finish, 2, D2)
+    ex.finish(2, D2)
     ex.complete(D1)
 
     def down_first(y, _):
@@ -444,18 +447,19 @@
     variate_ids,
     time_ids,
 ):
-    ffn_wide = jnp.pad(ffn_weight, ((0, 0), (0, 0), (0, 32)))
-    down_wide = jnp.pad(down_weight.T, ((0, 0), (0, 32)))
+    wide = jnp.pad(ffn_weight, ((0, 1), (0, 0), (0, 32))) + jnp.pad(
+        down_weight.T[None], ((2, 0), (0, 0), (0, 32))
+    )
     vmem = pl.BlockSpec(memory_space=pltpu.VMEM)
     hbm = pl.BlockSpec(memory_space=pl.ANY)
     smem = pl.BlockSpec(memory_space=pltpu.SMEM)
     buffers = [
-        pltpu.VMEM((128, ROWS[b][c], 128), BF) for b in range(5) for c in range(3)
+        pltpu.VMEM((128, START[5][c], 128), BF) for c in range(3)
     ]
     return pl.pallas_call(
         kernel,
-        out_shape=jax.ShapeDtypeStruct((L, D), BF),
-        in_specs=[hbm, vmem, hbm, hbm, hbm, hbm, vmem, smem, vmem, vmem, vmem],
+        out_shape=pltpu.VMEM((L, D), BF),
+        in_specs=[hbm, vmem, hbm, hbm, hbm, vmem, smem, vmem, vmem, vmem],
         out_specs=vmem,
         scratch_shapes=buffers
         + [
@@ -477,8 +481,8 @@
             pltpu.VMEM((L, D), F32),
             pltpu.SemaphoreType.DMA((5, 3, 2)),
             pltpu.SemaphoreType.DMA,
-            pltpu.SemaphoreType.DMA((5, 3, NS)),
-            pltpu.SemaphoreType.DMA((5, 3, NS)),
+            pltpu.SemaphoreType.DMA((SEMS,)),
+            pltpu.SemaphoreType.DMA((SEMS,)),
         ],
         compiler_params=pltpu.CompilerParams(
             collective_id=0, has_side_effects=True, vmem_limit_bytes=VMEM
@@ -488,8 +492,7 @@
         norm_gain,
         qkv_weight,
         out_weight.T,
-        ffn_wide,
-        down_wide,
+        wide,
         jnp.asarray(turn_table()),
         variate_bias,
         sample_ids.reshape(1, L),

time: 85.8 us -> 79.3 us (0.924)
  Pallas kernels: 81.3 us -> 76.6 us
  local copies, waits for them, and re-layouts: 4.38 us -> 0.97 us
  other arithmetic: 0 us -> 1.6 us
    pallas_call x1, Pallas kernels: 81.3 us -> 76.6 us  [local(): pl.pallas_call(kernel, out_shape=pltpu.VMEM((L, D), BF), in_specs=[hbm, v...]
    pad x2 -> x0, local copies, waits for them, and re-layouts: 2.11 us -> none  [the longest x1 1.45 us: local(): down_wide = jnp.pad(down_weight.T, ((0, 0), (0, 32)))]
    add x0 -> x1, other arithmetic: none -> 1.6 us  [local(): jnp.pad(ffn_weight, ((0, 1), (0, 0), (0, 32)))]
    unnamed x3 -> x1, local copies, waits for them, and re-layouts: 2.27 us -> 0.97 us
where the time goes in v2:
time: 79.3 us; the launch traced here: 79.2 us
  Pallas kernels  76.6 us (97%)
  other arithmetic  1.6 us (2%)
  local copies, waits for them, and re-layouts  0.97 us (1%)
    pallas_call x1, Pallas kernels, local(): pl.pallas_call(kernel, out_shape=pltpu.VMEM((L, D), BF), in_specs=[hbm, v...  76.6 us
    add x1, other arithmetic, local(): jnp.pad(ffn_weight, ((0, 1), (0, 0), (0, 32)))  1.6 us

profile of v2, /device:TPU:1, one launch (start us, length us, event | category | flops | bytes accessed | tf_op | source)
XLA Modules:
  0.0 79.2 jit_solution(11193644408516605932)
XLA Ops:
  0.0 1.6 %pad_add_fusion.wide = bf16[3,64,384]{2,1,0:T(8,128)(2,1)} fusion(bf16[1,64,352]{2,1,0:T(8,128)(2,1)} %bitcast.7, bf16[2,64,352]{2,1,0:T(8,128)(2,1)} %param.16), kind=kLoop, calls=%fused_computation | loop fusion | flops 294912 | bytes 282624 | tf_op jit(solution)/shard_map/add | solution.py:450
  1.6 76.6 %shard_map.109 = bf16[512,1024]{1,0:T(8,128)(2,1)S(1)} custom-call(bf16[512,1024]{1,0:T(8,128)(2,1)} %tok_hbm.1, f32[2,1024]{1,0:T(2,128)} %gain.1, bf16[3,64,128]{2,1,0:T(8,128)(2,1)} %qkvw.1, bf16[64,128]{1,0:T(8,128)(2,1)} %bitcast.8, bf16[3,64,384]{2,1,0:T(8,128)(2,1)} %pad_add_fusion.wide, bf16[128,768]{1,0:T(8,128)(2,1)} %constant.5.clone.table, ...), custom_call_target="tpu_custom_call" | custom-call | tf_op jit(solution)/shard_map/pallas_call | solution.py:459
  78.2 1.0 %copy.13 = bf16[512,1024]{1,0:T(8,128)(2,1)} copy(bf16[512,1024]{1,0:T(8,128)(2,1)S(1)} %shard_map.109) | data formatting | bytes 2097152
